TPU v7x, 32 devices: a whole 2x2x4 slice. The times are simulated.
32 devices in a mesh: grid: 8 (over z, y), atom: 4 (over x, core).
Axes of the slice: x: 2, y: 2, z: 4, core: 2. Of those that a mesh axis runs over, the one named last changes fastest.
Arguments:
- weights: float32 [524288], P(('grid', 'atom')), may hold values from 0.25 to 4
- target: float32 [524288], P(('grid', 'atom')), may hold values from -6 to 6
- coupling: float32 [524288], P(('grid', 'atom')), may hold values from -0.9 to 0.9
- multipole_basis: float32 [25, 524288], P(None, ('grid', 'atom')), may hold values from -6 to 6
- rho_hist: float32 [8, 524288], P(None, ('grid', 'atom')), may hold values from -6 to 6
- res_hist: float32 [8, 524288], P(None, ('grid', 'atom')), may hold values from -6 to 6
- batch_atom: int32 [2048], P(('grid', 'atom')), may hold values from 0 to 2047
- owner_slot: int32 [2048], replicated, may hold values from 0 to 2047, each once
- slot_index: int32 [2], replicated, may hold values from 0 to 7
Outputs:
- density: float32 [524288], P(('grid', 'atom'))
- moments: float32 [25, 2048], P(None, 'atom')
Inputs may be any that keep to these rules, and one draw needn't show every extreme that they name: `owner_slot`: each slot 0 to 2047 belongs to exactly one atom.
All inputs are finite; a program needn't handle non-finite values.
Results may differ from a plain program's by a relative error of at most 0.00011.
Values sent between devices are 32-bit elements; how exact they have to be, the bound alone decides.
A program may use at most 64 MiB of HBM per device.

v0:
```python
import math

import jax
import jax.numpy as jnp
import numpy as np
from jax import lax
from jax.sharding import PartitionSpec as P

ITERS = 2


damping_table = np.array(
    [1.0 / (1 + degree) for degree in range(5) for order in range(2 * degree + 1)], dtype=np.float32
)
mixing_beta = 0.5
ridge_share = 0.1


def mixing_weights(intersect):
    hist_len = intersect.shape[0]
    ridge_val = ridge_share * jnp.trace(intersect) / hist_len
    shifted = intersect + ridge_val * jnp.eye(hist_len, dtype=intersect.dtype)
    factor = jnp.linalg.cholesky(shifted)
    forward = []
    for row_at in range(hist_len):
        entry_val = 1.0
        for col_at in range(row_at):
            entry_val = entry_val - factor[row_at, col_at] * forward[col_at]
        forward.append(entry_val / factor[row_at, row_at])
    backward = [None] * hist_len
    for row_at in reversed(range(hist_len)):
        entry_val = forward[row_at]
        for col_at in range(row_at + 1, hist_len):
            entry_val = entry_val - factor[col_at, row_at] * backward[col_at]
        backward[row_at] = entry_val / factor[row_at, row_at]
    solved = jnp.stack(backward)
    return solved / jnp.sum(solved)


def joint_total(intersect_part, moment_part):
    return lax.psum((intersect_part, moment_part), ("grid", "atom"))


def local(
    weights,
    target,
    coupling,
    multipole_basis,
    rho_hist,
    res_hist,
    batch_atom,
    owner_slot,
    slot_index,
):
    hi_prec = lax.Precision.HIGHEST
    harmonics = multipole_basis.shape[0]
    points = weights.shape[0]
    batch_count = batch_atom.shape[0]
    batch_width = points // batch_count
    atom_total = owner_slot.shape[0]
    owned_count = atom_total // lax.axis_size("atom")
    atom_points = points * lax.axis_size("grid") // owned_count
    moment_scale = 1.0 / math.sqrt(atom_points)
    damping = jnp.asarray(damping_table, dtype=weights.dtype)
    batch_slot = owner_slot[batch_atom]
    one_hot = (batch_slot[:, None] == jnp.arange(atom_total, dtype=jnp.int32)[None, :]).astype(
        weights.dtype
    )
    basis_blocks = multipole_basis.reshape(harmonics, batch_count, batch_width)
    intersect = None
    hist_moments = None
    density = None
    owned_moms = None
    res_new = None
    previous = None
    for iteration in range(ITERS):
        intersect_part = jnp.dot(res_hist * weights[None, :], res_hist.T, precision=hi_prec)
        leading = res_hist.shape[0]
        weighted = (res_hist * weights[None, :]).reshape(leading, 1, batch_count, batch_width)
        per_batch = jnp.sum(weighted * basis_blocks[None], axis=3)
        summed = jnp.dot(
            per_batch.reshape(leading * harmonics, batch_count), one_hot, precision=hi_prec
        )
        intersect, hist_moments = joint_total(
            intersect_part, summed.reshape(leading, harmonics, atom_total) * moment_scale
        )
        coeffs = mixing_weights(intersect)
        res_mix = jnp.dot(coeffs, res_hist, precision=hi_prec)
        all_moments = jnp.tensordot(coeffs, hist_moments, axes=1, precision=hi_prec)
        owned_moms = lax.dynamic_slice_in_dim(
            all_moments, lax.axis_index("atom") * owned_count, owned_count, 1
        )
        rho_mix = jnp.dot(coeffs, rho_hist, precision=hi_prec)
        at_batch = jnp.dot(all_moments * damping[:, None], one_hot.T, precision=hi_prec)
        density = rho_mix + mixing_beta * (
            res_mix - jnp.sum(at_batch[:, :, None] * basis_blocks, axis=0).reshape(points)
        )
        res_new = target + coupling * jnp.tanh(density) - density
        previous = slot_index[iteration]
        rho_hist = rho_hist.at[previous].set(density)
        res_hist = res_hist.at[previous].set(res_new)
    return (density, owned_moms)


def solution(mesh):
    placed = (
        P(("grid", "atom")),
        P(("grid", "atom")),
        P(("grid", "atom")),
        P(None, ("grid", "atom")),
        P(None, ("grid", "atom")),
        P(None, ("grid", "atom")),
        P(("grid", "atom")),
        P(),
        P(),
    )
    return jax.shard_map(
        local,
        mesh=mesh,
        in_specs=placed,
        out_specs=(P(("grid", "atom")), P(None, "atom")),
        check_vma=False,
    )
```

profile of v0, /device:TPU:0, one launch (start us, length us, event | category | flops | bytes accessed | tf_op | source)
XLA Modules:
  0.0 317.4 jit_solution(1176447860668148398)
XLA Ops:
  7.2 0.0 all-reduce.3.cloned.1.call-start
  7.2 1.2 copy.59
  8.4 1.0 copy.58
  9.5 0.1 broadcast_multiply_fusion.1
  9.5 0.2 copy.26
  9.7 0.6 copy.36
  10.4 0.2 slice.398
  10.6 0.5 copy-done.9
  11.1 1.2 copy-done.2
  12.2 1.8 multiply_reduce_fusion.1
  14.0 0.8 gather_fusion
  14.8 2.3 convolution_multiply_fusion.1
  17.2 0.0 all-reduce.5.cloned.1.call-start
  17.2 1.2 fusion.15
  18.5 42.3 %psum.28 = f32[8,8]{0,1:T(8,128)S(1)} all-reduce(f32[8,8]{0,1:T(8,128)S(1)} %fusion.15), channel_id=1, replica_groups=mesh['grid'=8,'atom'=4] {'grid','atom'}, use_global_device_ids=true, to_apply=%region_1.0 | all-reduce | flops 64 | bytes 512 | tf_op jit(solution)/shard_map/psum | solution.py:41
  60.7 0.6 select_reduce_fusion.2
  62.0 0.1 copy.25
  62.1 0.7 cholesky.44
  62.8 0.6 compare_reduce_fusion.1
  63.5 0.6 fusion.23
  64.1 0.7 fusion.37
  73.7 0.7 fusion.36
  111.2 0.1 stack.62
  111.3 0.7 and_reduce_fusion
  112.0 0.6 fusion.30
  112.6 0.6 fusion.32
  113.2 41.8 %all-reduce.3.cloned.1.call-done = f32[8,25,2048]{2,1,0:T(8,128)} async-done(((f32[8,25,2048]{2,1,0:T(8,128)}), f32[8,25,2048]{2,1,0:T(8,128)}) %all-reduce.3.cloned.1.call-update) | async-done | bytes 1638416 | tf_op jit(solution)/shard_map/psum | solution.py:41
  154.9 3.8 %fusion.2 = f32[1,25,2048]{2,0,1:T(1,128)S(1)} fusion(f32[8,25,2048]{2,1,0:T(8,128)} %all-reduce.3.cloned.1.call-done, f32[8]{0:T(128)S(1)} %stack.62, f32[]{:T(128)S(6)} %reduce_sum.109), kind=kOutput, calls=%fused_computation.9 | convolution fusion | flops 4915208 | bytes 1843236 | tf_op jit(solution)/shard_map/dot_general | solution.py:89
  158.8 0.5 fusion.5
  159.3 0.3 mul.524
  159.6 0.2 pad.7
  159.8 1.2 copy.37
  161.0 0.4 multiply_reduce_fusion.3
  161.5 0.4 copy-done.5
  161.9 0.0 copy-done.6
  161.9 0.8 broadcast_select_fusion
  162.7 0.5 scatter.6
  163.2 0.1 broadcast_multiply_fusion
  163.3 1.2 fusion.16
  164.5 0.2 copy.29
  164.7 1.8 multiply_reduce_fusion
  166.5 2.3 convolution_multiply_fusion
  168.9 39.6 %psum.30 = f32[8,8]{0,1:T(8,128)S(1)} all-reduce(f32[8,8]{0,1:T(8,128)S(1)} %fusion.16), channel_id=1, replica_groups=mesh['grid'=8,'atom'=4] {'grid','atom'}, use_global_device_ids=true, to_apply=%region_8.10 | all-reduce | flops 64 | bytes 512 | tf_op jit(solution)/shard_map/psum | solution.py:41
  208.4 0.6 select_reduce_fusion.1
  209.7 0.1 copy.28
  209.8 0.7 cholesky.55
  210.5 0.6 compare_reduce_fusion
  211.2 0.6 select_select_fusion
  211.8 0.7 fusion.35
  221.5 0.7 fusion.34
  258.9 0.5 scatter.9
  259.4 0.1 stack.71
  259.5 0.6 fusion.25
  260.1 0.6 fusion.27
  260.7 42.0 %all-reduce.5.cloned.1.call-done = f32[8,25,2048]{2,1,0:T(8,128)} async-done(((f32[8,25,2048]{2,1,0:T(8,128)}), f32[8,25,2048]{2,1,0:T(8,128)}) %all-reduce.5.cloned.1.call-update) | async-done | bytes 1638416 | tf_op jit(solution)/shard_map/psum | solution.py:41
  302.7 3.8 %fusion = f32[1,25,2048]{2,0,1:T(1,128)S(1)} fusion(f32[8,25,2048]{2,1,0:T(8,128)} %all-reduce.5.cloned.1.call-done, f32[8]{0:T(128)S(1)} %stack.71, f32[]{:T(128)S(6)} %reduce_sum.119), kind=kOutput, calls=%fused_computation.7 | convolution fusion | flops 4915208 | bytes 1843236 | tf_op jit(solution)/shard_map/dot_general | solution.py:89
  306.5 0.5 fusion.4
  307.0 0.1 copy.51
  307.1 0.3 mul.593
  307.3 0.2 pad.8
  307.6 1.2 copy.38
  308.8 0.4 multiply_reduce_fusion.2
  309.2 0.6 constant_dynamic-slice_fusion
  309.9 0.6 multiply_add_fusion
  (29 shorter events, 0.3 us)
Async XLA Ops:
  7.2 6.8 %copy-start = (s32[2048]{0:T(1024)S(1)}, s32[2048]{0:T(1024)}, u32[]{:S(2)}) copy-start(s32[2048]{0:T(1024)} %param.22) | copy-start | bytes 24580
  7.2 2.3 copy-start.4
  7.2 2.5 copy-start.1
  7.2 147.7 %all-reduce.3.cloned.1.call-start = ((), (), s32[]{:S(2)}) async-start(), calls=%async_computation | async-start | bytes 4194304 | tf_op jit(solution)/shard_map/psum | solution.py:41
  10.4 0.7 copy-start.9
  11.0 1.2 copy-start.2
  17.1 94.0 %copy-start.7 = (s32[2]{0:T(128)S(1)}, s32[2]{0:T(128)}, u32[]{:S(2)}) copy-start(s32[2]{0:T(128)} %param.23) | copy-start | bytes 28
  17.1 94.2 %copy-start.8 = (s32[2]{0:T(128)S(1)}, s32[2]{0:T(128)}, u32[]{:S(2)}) copy-start(s32[2]{0:T(128)} %constant.99.clone.1) | copy-start | bytes 28
  17.2 141.6 %copy-start.10 = (f32[25]{0:T(128)S(1)}, f32[25]{0:T(128)}, u32[]{:S(2)}) copy-start(f32[25]{0:T(128)} %constant.108.clone) | copy-start | bytes 304
  17.2 285.5 %all-reduce.5.cloned.1.call-start = ((), (), s32[]{:S(2)}) async-start(), calls=%async_computation.1 | async-start | bytes 4194304 | tf_op jit(solution)/shard_map/psum | solution.py:41
  161.0 0.8 copy-start.5
  161.0 0.9 copy-start.6
  163.2 1.5 copy-start.3
Sparse Core Ops, SparseCore 0:
  17.3 137.6 all-reduce.2
  169.0 133.6 all-reduce.4
where the time goes:
time: 319 us; the launch traced here: 317 us
  between operations  107 us (34%)
  waiting for transfers between devices  83.7 us (26%)
  blocking collectives  81.8 us (26%)
  matrix products  18.1 us (6%)
  local copies, waits for them, and re-layouts  14.5 us (5%)
  other arithmetic  12 us (4%)
    psum x2, waiting for transfers between devices, joint_total(): return lax.psum((intersect_part, moment_part), ('grid', 'atom'))  83.7 us
    psum x2, blocking collectives, joint_total(): return lax.psum((intersect_part, moment_part), ('grid', 'atom'))  81.8 us
    unnamed x29, local copies, waits for them, and re-layouts  7.88 us
    dot_general x2, matrix products, local(): all_moments = jnp.tensordot(coeffs, hist_moments, axes=1, precision=hi_prec)  7.67 us
  transfers between devices with their start and end apart: 2, of which 2 were waited for; matrix products, arithmetic and copies ran while one was open for 4% of the time, Pallas kernels for 0%

commit v1 on v0

v1 whole, which is shorter than its diff:
```python
import functools
import math

import jax
import jax.numpy as jnp
from jax import lax
from jax.experimental import pallas as pl
from jax.experimental.pallas import tpu as pltpu
from jax.sharding import PartitionSpec as P

MESH = pl.DeviceIdType.MESH
LANES = 128
SUBS = 8
mixing_beta = 0.5
ridge_share = 0.1
F32 = jnp.float32


def solve_coeffs(entry, hist_len):
    trace = entry[0][0]
    for i in range(1, hist_len):
        trace = trace + entry[i][i]
    ridge = (ridge_share / hist_len) * trace
    low = [[entry[i][j] for j in range(i + 1)] for i in range(hist_len)]
    for i in range(hist_len):
        low[i][i] = low[i][i] + ridge
    inverse = [None] * hist_len
    factor = [[None] * hist_len for _ in range(hist_len)]
    forward = [jnp.ones_like(trace) for _ in range(hist_len)]
    for j in range(hist_len):
        inverse[j] = 1.0 / low[j][j]
        for i in range(j + 1, hist_len):
            factor[i][j] = low[i][j] * inverse[j]
        for i in range(j + 1, hist_len):
            forward[i] = forward[i] - factor[i][j] * forward[j]
            for k in range(j + 1, i + 1):
                low[i][k] = low[i][k] - factor[i][j] * low[k][j]
    backward = [forward[i] * inverse[i] for i in range(hist_len)]
    for j in reversed(range(hist_len)):
        for i in range(j):
            backward[i] = backward[i] - factor[j][i] * backward[j]
    total = backward[0]
    for i in range(1, hist_len):
        total = total + backward[i]
    return [backward[i] / total for i in range(hist_len)]


def kernel(
    cfg,
    batch_atom,
    owner_slot,
    slot_index,
    w_hbm,
    target_hbm,
    coupling_hbm,
    basis_hbm,
    rho_hbm,
    res_hbm,
    density_out,
    moments_out,
    w,
    target,
    coupling,
    basis,
    rho,
    res,
    fresh,
    fresh_w,
    row_bufs,
    moment_bufs,
    masks,
    mixed,
    load_sem,
    send_sem,
    recv_sem,
):
    iters, hist_len, harmonics, batches, width, owned, groups, members, scale = cfg
    devices = groups * members
    tiles = w.shape[0]
    per_batch = width // LANES
    half = LANES // 2
    pairs = devices // 2
    my_group = lax.axis_index("grid")
    my_member = lax.axis_index("atom")
    me = my_group * members + my_member

    def peer(step):
        spot = lax.rem(me + step, devices)
        return spot, (lax.div(spot, members), lax.rem(spot, members))

    barrier = pltpu.get_barrier_semaphore()

    @pl.loop(1, devices)
    def _(step):
        pl.semaphore_signal(barrier, inc=1, device_id=peer(step)[1], device_id_type=MESH)

    loads = [
        pltpu.make_async_copy(src, dst, load_sem.at[k])
        for k, (src, dst) in enumerate(
            ((res_hbm, res), (w_hbm, w), (basis_hbm, basis), (rho_hbm, rho), (target_hbm, target), (coupling_hbm, coupling))
        )
    ]
    for load in loads:
        load.start()

    lane = lax.broadcasted_iota(jnp.int32, (SUBS, LANES), 1)
    sub = lax.broadcasted_iota(jnp.int32, (SUBS, LANES), 0)
    lane_row = lax.broadcasted_iota(jnp.int32, (1, LANES), 1)

    slot_row = jnp.zeros((1, LANES), F32)
    slot_cols = []
    for block in range(batches // SUBS):
        col = jnp.zeros((SUBS, LANES), F32)
        for at in range(SUBS):
            b = block * SUBS + at
            slot = owner_slot[batch_atom[b]].astype(F32)
            slot_row = jnp.where(lane_row == half + b, slot, slot_row)
            col = jnp.where(sub == at, slot, col)
        slot_cols.append(col)
    slot_col = jnp.concatenate(slot_cols, axis=0)

    def lane_tile(t):
        return pl.ds(pl.multiple_of(t * LANES, LANES), LANES)

    def exchange(buf, which):
        def copy(step, spot):
            dst, device = peer(step)
            return pltpu.make_async_remote_copy(
                src_ref=buf.at[me],
                dst_ref=buf.at[spot],
                send_sem=send_sem.at[which, step],
                recv_sem=recv_sem.at[which, spot],
                device_id=device,
                device_id_type=MESH,
            )

        @pl.loop(1, devices)
        def _(step):
            copy(step, me).start()

        def wait():
            @pl.loop(1, devices)
            def _(step):
                copy(step, lax.rem(me - step + devices, devices)).wait_recv()

            @pl.loop(1, devices)
            def _(step):
                copy(step, me).wait_send()

        return wait

    def total_row(buf):
        total = buf[0]
        for spot in range(1, devices):
            total = total + buf[spot]
        return total

    def splat(row, k):
        return jnp.broadcast_to(row[:, k : k + 1], (1, LANES))

    shifts = hist_len // 2 + 1
    entry = None
    for iteration in range(iters):
        row_buf = row_bufs.at[iteration]
        moment_buf = moment_bufs.at[iteration]
        last = iteration == iters - 1

        if iteration == 0:
            loads[0].wait()
            loads[1].wait()

            def gram(step, acc):
                acc = list(acc)
                for u in range(8):
                    t = step * 8 + u
                    x = res[:, lane_tile(t)]
                    y = x * w[pl.ds(t, 1), :]
                    for r in range(shifts):
                        acc[r] = acc[r] + y * (pltpu.roll(x, r, 0) if r else x)
                return tuple(acc)

            acc = lax.fori_loop(0, tiles // 8, gram, tuple(jnp.zeros((SUBS, LANES), F32) for _ in range(shifts)))
            packed = jnp.zeros((SUBS, LANES), F32)
            for r in range(shifts):
                packed = jnp.where(lane == hist_len * r + sub, jnp.sum(acc[r], axis=1, keepdims=True), packed)
            row_buf[pl.ds(me, 1)] = (jnp.sum(packed, axis=0, keepdims=True) + slot_row)[None]
            pl.semaphore_wait(barrier, devices - 1)
        else:
            if iteration == 1:
                pass
            slot = slot_index[iteration - 1]
            replaced = sub == slot

            def refresh(step, acc):
                for u in range(8):
                    t = step * 8 + u
                    new_res = jnp.where(replaced, fresh[pl.ds(t, 1), :], res[:, lane_tile(t)])
                    new_rho = jnp.where(replaced, density_out[pl.ds(t, 1), :], rho[:, lane_tile(t)])
                    res[:, lane_tile(t)] = new_res
                    rho[:, lane_tile(t)] = new_rho
                    acc = acc + fresh_w[pl.ds(t, 1), :] * new_res
                return acc

            acc = lax.fori_loop(0, tiles // 8, refresh, jnp.zeros((SUBS, LANES), F32))
            packed = jnp.where(lane == sub, jnp.sum(acc, axis=1, keepdims=True), 0.0)
            row_buf[pl.ds(me, 1)] = jnp.sum(packed, axis=0, keepdims=True)[None]
        exchange(row_buf, 2 * iteration)()

        row = total_row(row_buf)
        if iteration == 0:
            entry = [[None] * (i + 1) for i in range(hist_len)]
            for i in range(hist_len):
                for j in range(i + 1):
                    r = i - j
                    at = hist_len * r + i if r < shifts else hist_len * (hist_len - r) + j
                    entry[i][j] = splat(row, at)
        else:
            news = [splat(row, k) for k in range(hist_len)]
            slot_vec = jnp.zeros((1, LANES), jnp.int32) + slot
            entry = [
                [
                    jnp.where(slot_vec == i, news[j], jnp.where(slot_vec == j, news[i], entry[i][j]))
                    for j in range(i + 1)
                ]
                for i in range(hist_len)
            ]
        coeffs = solve_coeffs(entry, hist_len)
        coeff_col = jnp.zeros((SUBS, LANES), F32)
        for i in range(hist_len):
            coeff_col = jnp.where(sub == i, coeffs[i], coeff_col)

        if iteration == 0:
            loads[2].wait()

        def moment_step(step, acc):
            lo, hi = acc
            for u in range(4):
                b = step * 4 + u
                parts = [None] * 4
                for v in range(per_batch):
                    t = b * per_batch + v
                    x = jnp.sum(coeff_col * res[:, lane_tile(t)], axis=0, keepdims=True) * w[pl.ds(t, 1), :]
                    for g in range(4):
                        rows = basis[g * SUBS : (g + 1) * SUBS, lane_tile(t)] if g < 3 else basis[24:25, lane_tile(t)]
                        term = rows * x
                        parts[g] = term if v == 0 else parts[g] + term
                sums = [jnp.sum(part, axis=1, keepdims=True) for part in parts]
                lo = jnp.where(lane == b, sums[0], jnp.where(lane == b + half, sums[2], lo))
                hi = jnp.where(lane == b, sums[1], jnp.where(lane == b + half, sums[3], hi))
            return lo, hi

        zero = jnp.zeros((SUBS, LANES), F32)
        lo, hi = lax.fori_loop(0, batches // 4, moment_step, (zero, zero))
        moment_buf[pl.ds(me, 1)] = jnp.concatenate([lo, hi], axis=0)[None]
        wait = exchange(moment_buf, 2 * iteration + 1)

        if iteration == 0:
            base = (my_member * owned).astype(F32)
            wide = lax.broadcasted_iota(jnp.int32, (owned, LANES), 0).astype(F32) + base

            @pl.loop(0, pairs)
            def _(q):
                even = row_buf[2 * q]
                odd = row_buf[2 * q + 1]
                slots = jnp.where(lane_row < half, pltpu.roll(even, half, 1), odd)
                masks[0:batches, lane_tile(q)] = jnp.where(slot_col == slots, 1.0, 0.0).astype(jnp.bfloat16)
                masks[batches : batches + owned, lane_tile(q)] = jnp.where(wide == slots, 1.0, 0.0).astype(jnp.bfloat16)

            for load in loads[3:]:
                load.wait()
        wait()

        lane16 = lax.broadcasted_iota(jnp.int32, (2 * SUBS, LANES), 1)

        @pl.loop(0, pairs)
        def _(q):
            even = moment_buf[2 * q]
            odd = moment_buf[2 * q + 1]
            first = jnp.where(lane16 < half, even, pltpu.roll(odd, half, 1))
            second = jnp.where(lane16 < half, pltpu.roll(even, half, 1), odd)
            rest = jnp.concatenate([first, second], axis=0)
            for part in range(3):
                piece = rest.astype(jnp.bfloat16)
                mixed[part * 32 : (part + 1) * 32, lane_tile(q)] = piece
                rest = rest - piece.astype(F32)

        def gathered(start, count):
            out = lax.dot_general(
                mixed[...], masks[start : start + count, :], (((1,), (1,)), ((), ())), preferred_element_type=F32
            )
            return (out[0:32] + out[32:64] + out[64:96]) * scale

        at_batch = gathered(0, batches)
        comp = lax.broadcasted_iota(jnp.int32, (32, batches), 0)
        degree = sum((comp >= (l + 1) * (l + 1)).astype(F32) for l in range(4))
        damped = jnp.where(comp < harmonics, at_batch * (mixing_beta / (1.0 + degree)), 0.0)
        lane_b = lax.broadcasted_iota(jnp.int32, (32, batches), 1)

        def density_step(step, carry):
            for u in range(4):
                b = step * 4 + u
                col = jnp.sum(jnp.where(lane_b == b, damped, 0.0), axis=1, keepdims=True)
                for v in range(per_batch):
                    t = b * per_batch + v
                    part = coeff_col * (rho[:, lane_tile(t)] + mixing_beta * res[:, lane_tile(t)])
                    for g in range(3):
                        part = part - col[g * SUBS : (g + 1) * SUBS] * basis[g * SUBS : (g + 1) * SUBS, lane_tile(t)]
                    part = part - col[24:32] * basis[24:25, lane_tile(t)]
                    density_out[pl.ds(t, 1), :] = jnp.sum(part, axis=0, keepdims=True)
            return carry

        lax.fori_loop(0, batches // 4, density_step, 0)
        if last:
            moments_out[...] = gathered(batches, owned)[0:harmonics]
        else:
            density = density_out[...]
            new = target[...] + coupling[...] * jnp.tanh(density) - density
            fresh[...] = new
            fresh_w[...] = new * w[...]


def local(weights, target, coupling, multipole_basis, rho_hist, res_hist, batch_atom, owner_slot, slot_index):
    harmonics, points = multipole_basis.shape
    hist_len = res_hist.shape[0]
    batches = batch_atom.shape[0]
    groups = lax.axis_size("grid")
    members = lax.axis_size("atom")
    devices = groups * members
    owned = owner_slot.shape[0] // members
    scale = 1.0 / math.sqrt(points * groups // owned)
    iters = slot_index.shape[0]
    cfg = (iters, hist_len, harmonics, batches, points // batches, owned, groups, members, scale)
    tiles = points // LANES
    flat = (tiles, LANES)
    any_space = pl.BlockSpec(memory_space=pl.ANY)
    smem = pl.BlockSpec(memory_space=pltpu.SMEM)
    vmem = pl.BlockSpec(memory_space=pltpu.VMEM)
    density, moments = pl.pallas_call(
        functools.partial(kernel, cfg),
        out_shape=(jax.ShapeDtypeStruct(flat, F32), jax.ShapeDtypeStruct((harmonics, owned), F32)),
        in_specs=[smem] * 3 + [any_space] * 6,
        out_specs=(vmem, vmem),
        scratch_shapes=[
            pltpu.VMEM(flat, F32),
            pltpu.VMEM(flat, F32),
            pltpu.VMEM(flat, F32),
            pltpu.VMEM((harmonics, points), F32),
            pltpu.VMEM((hist_len, points), F32),
            pltpu.VMEM((hist_len, points), F32),
            pltpu.VMEM(flat, F32),
            pltpu.VMEM(flat, F32),
            pltpu.VMEM((iters, devices, 1, LANES), F32),
            pltpu.VMEM((iters, devices, 2 * SUBS, LANES), F32),
            pltpu.VMEM((batches + owned, devices * batches), jnp.bfloat16),
            pltpu.VMEM((96, devices * batches), jnp.bfloat16),
            pltpu.SemaphoreType.DMA((6,)),
            pltpu.SemaphoreType.DMA((2 * iters, devices)),
            pltpu.SemaphoreType.DMA((2 * iters, devices)),
        ],
        compiler_params=pltpu.CompilerParams(
            collective_id=0, has_side_effects=True, vmem_limit_bytes=48 * 1024 * 1024
        ),
    )(
        batch_atom,
        owner_slot,
        slot_index,
        weights.reshape(flat),
        target.reshape(flat),
        coupling.reshape(flat),
        multipole_basis,
        rho_hist,
        res_hist,
    )
    return density.reshape(points), moments


def solution(mesh):
    both = ("grid", "atom")
    placed = (P(both), P(both), P(both), P(None, both), P(None, both), P(None, both), P(both), P(), P())
    return jax.shard_map(
        local,
        mesh=mesh,
        in_specs=placed,
        out_specs=(P(both), P(None, "atom")),
        check_vma=False,
    )
```

time: 319 us -> 55 us (0.17)
  between operations: 107 us -> 0.66 us
  waiting for transfers between devices: 83.7 us -> 0 us
  blocking collectives: 81.8 us -> 0 us
  Pallas kernels: 0 us -> 44.4 us
  matrix products: 18.1 us -> 0 us
  other arithmetic: 12 us -> 0 us
  local copies, waits for them, and re-layouts: 14.5 us -> 9.45 us
    psum x2 -> x0, waiting for transfers between devices: 83.7 us -> none  [joint_total(): return lax.psum((intersect_part, moment_part), ('grid', 'atom'))]
    psum x2 -> x0, blocking collectives: 81.8 us -> none  [joint_total(): return lax.psum((intersect_part, moment_part), ('grid', 'atom'))]
    pallas_call x0 -> x1, Pallas kernels: none -> 44.4 us  [local(): pl.pallas_call(functools.partial(kernel, cfg), out_shape=(jax.ShapeDtypeS...]
    dot_general x12 -> x0, matrix products: 18.1 us -> none  [the longest x2 7.67 us: local(): all_moments = jnp.tensordot(coeffs, hist_moments, axes=1, precision=hi_prec)]
    reduce_sum x6 -> x0, other arithmetic: 5.6 us -> none  [the longest x2 3.53 us: local(): per_batch = jnp.sum(weighted * basis_blocks[None], axis=3)]
    another operation x8 -> x0, other arithmetic: 4.3 us -> none  [the longest x6 2.79 us: mixing_weights(): factor = jnp.linalg.cholesky(shifted)]
    unnamed x29 -> x20, local copies, waits for them, and re-layouts: 7.88 us -> 9.45 us
  transfers between devices with their start and end apart: 2 -> 0, of which waited for: 2 -> 0; matrix products, arithmetic and copies ran while one was open for 4% -> 0% of each run, Pallas kernels for 0% -> 0%
where the time goes in v1:
time: 55 us; the launch traced here: 54.5 us
  Pallas kernels  44.4 us (81%)
  local copies, waits for them, and re-layouts  9.45 us (17%)
  between operations  0.66 us (1%)
    pallas_call x1, Pallas kernels, local(): pl.pallas_call(functools.partial(kernel, cfg), out_shape=(jax.ShapeDtypeS...  44.4 us
    unnamed x20, local copies, waits for them, and re-layouts  9.45 us

profile of v1, /device:TPU:0, one launch (start us, length us, event | category | flops | bytes accessed | tf_op | source)
XLA Modules:
  0.0 54.5 jit_solution(15817262617284621946)
XLA Ops:
  0.6 0.0 copy-start
  0.6 1.6 %copy-done = f32[25,16384]{1,0:T(8,128)S(1)} copy-done((f32[25,16384]{1,0:T(8,128)S(1)}, f32[25,16384]{1,0:T(8,128)}, u32[]{:S(2)}) %copy-start) | copy-done | bytes 1638424
  2.2 0.0 copy-start.1
  2.2 1.0 %copy-done.1 = f32[8,16384]{1,0:T(8,128)S(1)} copy-done((f32[8,16384]{1,0:T(8,128)S(1)}, f32[8,16384]{1,0:T(8,128)}, u32[]{:S(2)}) %copy-start.1) | copy-done | bytes 524312
  3.3 0.0 copy-start.2
  3.3 1.0 %copy-done.2 = f32[8,16384]{1,0:T(8,128)S(1)} copy-done((f32[8,16384]{1,0:T(8,128)S(1)}, f32[8,16384]{1,0:T(8,128)}, u32[]{:S(2)}) %copy-start.2) | copy-done | bytes 524312
  4.3 0.0 copy-start.3
  4.3 0.8 %copy-done.3 = f32[16384]{0:T(1024)S(1)} copy-done((f32[16384]{0:T(1024)S(1)}, f32[16384]{0:T(1024)}, u32[]{:S(2)}) %copy-start.3) | copy-done | bytes 65560
  5.1 0.0 copy-start.4
  5.2 0.8 %copy-done.4 = f32[16384]{0:T(1024)S(1)} copy-done((f32[16384]{0:T(1024)S(1)}, f32[16384]{0:T(1024)}, u32[]{:S(2)}) %copy-start.4) | copy-done | bytes 65560
  6.0 0.0 copy-start.5
  6.0 0.8 %copy-done.5 = f32[16384]{0:T(1024)S(1)} copy-done((f32[16384]{0:T(1024)S(1)}, f32[16384]{0:T(1024)}, u32[]{:S(2)}) %copy-start.5) | copy-done | bytes 65560
  6.8 0.0 copy-start.6
  6.8 0.7 %copy-done.6 = s32[2048]{0:T(1024)S(1)} copy-done((s32[2048]{0:T(1024)S(1)}, s32[2048]{0:T(1024)}, u32[]{:S(2)}) %copy-start.6) | copy-done | bytes 8216
  7.5 0.0 copy-start.7
  7.5 0.7 %copy-done.7 = s32[64]{0:T(128)S(1)} copy-done((s32[64]{0:T(128)S(1)}, s32[64]{0:T(128)}, u32[]{:S(2)}) %copy-start.7) | copy-done | bytes 280
  8.2 0.0 copy-start.8
  8.2 0.7 %copy-done.8 = s32[2]{0:T(128)S(1)} copy-done((s32[2]{0:T(128)S(1)}, s32[2]{0:T(128)}, u32[]{:S(2)}) %copy-start.8) | copy-done | bytes 32
  8.8 44.4 %shard_map.104 = (f32[128,128]{1,0:T(8,128)S(1)}, f32[25,512]{1,0:T(8,128)S(1)}) custom-call(s32[64]{0:T(128)S(1)} %copy-done.7, s32[2048]{0:T(1024)S(1)} %copy-done.6, s32[2]{0:T(128)S(1)} %copy-done.8, f32[128,128]{1,0:T(8,128)S(1)} %bitcast.4, f32[128,128]{1,0:T(8,128)S(1)} %bitcast.5, f32[128,128]{1,0:T(8,128)S(1)} %bitcast.6, f32[25,16384]{1,0:T(8,128)S(1)} %copy-done, ...), custom_call_target="tpu_custom_call" | custom-call | tf_op jit(solution)/shard_map/pallas_call | solution.py:338
  53.3 0.6 %copy.13 = f32[16384]{0:T(1024)} copy(f32[16384]{0:T(1024)S(1)} %bitcast.7) | data formatting | bytes 131072
  53.9 0.6 %copy.14 = f32[25,512]{1,0:T(8,128)} copy(f32[25,512]{1,0:T(8,128)S(1)} %get-tuple-element.9) | data formatting | bytes 102400
Async XLA Ops:
  0.6 1.6 %copy-start = (f32[25,16384]{1,0:T(8,128)S(1)}, f32[25,16384]{1,0:T(8,128)}, u32[]{:S(2)}) copy-start(f32[25,16384]{1,0:T(8,128)} %basis_hbm.1) | copy-start | bytes 4915204
  2.2 1.0 %copy-start.1 = (f32[8,16384]{1,0:T(8,128)S(1)}, f32[8,16384]{1,0:T(8,128)}, u32[]{:S(2)}) copy-start(f32[8,16384]{1,0:T(8,128)} %rho_hbm.1) | copy-start | bytes 1572868
  3.3 1.0 %copy-start.2 = (f32[8,16384]{1,0:T(8,128)S(1)}, f32[8,16384]{1,0:T(8,128)}, u32[]{:S(2)}) copy-start(f32[8,16384]{1,0:T(8,128)} %res_hbm.1) | copy-start | bytes 1572868
  4.3 0.8 %copy-start.3 = (f32[16384]{0:T(1024)S(1)}, f32[16384]{0:T(1024)}, u32[]{:S(2)}) copy-start(f32[16384]{0:T(1024)} %param.9) | copy-start | bytes 196612
  5.1 0.8 %copy-start.4 = (f32[16384]{0:T(1024)S(1)}, f32[16384]{0:T(1024)}, u32[]{:S(2)}) copy-start(f32[16384]{0:T(1024)} %param.10) | copy-start | bytes 196612
  6.0 0.8 %copy-start.5 = (f32[16384]{0:T(1024)S(1)}, f32[16384]{0:T(1024)}, u32[]{:S(2)}) copy-start(f32[16384]{0:T(1024)} %param.11) | copy-start | bytes 196612
  6.8 0.7 %copy-start.6 = (s32[2048]{0:T(1024)S(1)}, s32[2048]{0:T(1024)}, u32[]{:S(2)}) copy-start(s32[2048]{0:T(1024)} %owner_slot.1) | copy-start | bytes 24580
  7.5 0.7 %copy-start.7 = (s32[64]{0:T(128)S(1)}, s32[64]{0:T(128)}, u32[]{:S(2)}) copy-start(s32[64]{0:T(128)} %batch_atom.1) | copy-start | bytes 772
  8.2 0.7 %copy-start.8 = (s32[2]{0:T(128)S(1)}, s32[2]{0:T(128)}, u32[]{:S(2)}) copy-start(s32[2]{0:T(128)} %slot_index.1) | copy-start | bytes 28

commit v2 on v1

--- a/solution.py
+++ b/solution.py
@@ -45,6 +45,15 @@
     return [backward[i] / total for i in range(hist_len)]
 
 
+def split(x):
+    pieces = []
+    for _ in range(3):
+        piece = x.astype(jnp.bfloat16).astype(F32)
+        pieces.append(piece)
+        x = x - piece
+    return pieces
+
+
 def kernel(
     cfg,
     batch_atom,
@@ -68,8 +77,11 @@
     fresh_w,
     row_bufs,
     moment_bufs,
-    masks,
-    mixed,
+    near,
+    own,
+    hist_moments,
+    base_rows,
+    correct,
     load_sem,
     send_sem,
     recv_sem,
@@ -79,7 +91,7 @@
     tiles = w.shape[0]
     per_batch = width // LANES
     half = LANES // 2
-    pairs = devices // 2
+    rows = batches // 4
     my_group = lax.axis_index("grid")
     my_member = lax.axis_index("atom")
     me = my_group * members + my_member
@@ -105,6 +117,7 @@
 
     lane = lax.broadcasted_iota(jnp.int32, (SUBS, LANES), 1)
     sub = lax.broadcasted_iota(jnp.int32, (SUBS, LANES), 0)
+    quarter = lane // 32
     lane_row = lax.broadcasted_iota(jnp.int32, (1, LANES), 1)
 
     slot_row = jnp.zeros((1, LANES), F32)
@@ -186,8 +199,6 @@
             row_buf[pl.ds(me, 1)] = (jnp.sum(packed, axis=0, keepdims=True) + slot_row)[None]
             pl.semaphore_wait(barrier, devices - 1)
         else:
-            if iteration == 1:
-                pass
             slot = slot_index[iteration - 1]
             replaced = sub == slot
 
@@ -204,7 +215,34 @@
             acc = lax.fori_loop(0, tiles // 8, refresh, jnp.zeros((SUBS, LANES), F32))
             packed = jnp.where(lane == sub, jnp.sum(acc, axis=1, keepdims=True), 0.0)
             row_buf[pl.ds(me, 1)] = jnp.sum(packed, axis=0, keepdims=True)[None]
-        exchange(row_buf, 2 * iteration)()
+        wait = exchange(row_buf, 2 * iteration)
+
+        if iteration == 0:
+            loads[2].wait()
+
+        @pl.loop(0, rows)
+        def _(r):
+            xs, ys = [], []
+            for q in range(4):
+                b = q * rows + r
+                at = pl.ds(pl.multiple_of(b * width, width), width)
+                gain = jnp.concatenate([w[pl.ds(b * per_batch + v, 1), :] for v in range(per_batch)], axis=1)
+                xs.extend(split(res[:, at] * gain))
+                ys.append(jnp.concatenate([basis[0:24, at], jnp.broadcast_to(basis[24:25, at], (SUBS, width))], axis=0))
+            x = jnp.concatenate(xs, axis=0).astype(jnp.bfloat16)
+            out = None
+            for y in split(jnp.concatenate(ys, axis=0)):
+                part = lax.dot_general(
+                    x, y.astype(jnp.bfloat16), (((1,), (1,)), ((), ())), preferred_element_type=F32
+                )
+                out = part if out is None else out + part
+            tile = jnp.zeros((SUBS, LANES), F32)
+            for q in range(4):
+                block = out[24 * q : 24 * q + 8] + out[24 * q + 8 : 24 * q + 16] + out[24 * q + 16 : 24 * q + 24]
+                tile = jnp.where(quarter == q, block, tile)
+            hist_moments[r] = tile
+
+        wait()
 
         row = total_row(row_buf)
         if iteration == 0:
@@ -229,68 +267,56 @@
         for i in range(hist_len):
             coeff_col = jnp.where(sub == i, coeffs[i], coeff_col)
 
-        if iteration == 0:
-            loads[2].wait()
-
-        def moment_step(step, acc):
-            lo, hi = acc
-            for u in range(4):
-                b = step * 4 + u
-                parts = [None] * 4
-                for v in range(per_batch):
-                    t = b * per_batch + v
-                    x = jnp.sum(coeff_col * res[:, lane_tile(t)], axis=0, keepdims=True) * w[pl.ds(t, 1), :]
-                    for g in range(4):
-                        rows = basis[g * SUBS : (g + 1) * SUBS, lane_tile(t)] if g < 3 else basis[24:25, lane_tile(t)]
-                        term = rows * x
-                        parts[g] = term if v == 0 else parts[g] + term
-                sums = [jnp.sum(part, axis=1, keepdims=True) for part in parts]
-                lo = jnp.where(lane == b, sums[0], jnp.where(lane == b + half, sums[2], lo))
-                hi = jnp.where(lane == b, sums[1], jnp.where(lane == b + half, sums[3], hi))
-            return lo, hi
-
-        zero = jnp.zeros((SUBS, LANES), F32)
-        lo, hi = lax.fori_loop(0, batches // 4, moment_step, (zero, zero))
-        moment_buf[pl.ds(me, 1)] = jnp.concatenate([lo, hi], axis=0)[None]
+        mixed = [jnp.sum(coeff_col * hist_moments[r], axis=0, keepdims=True) for r in range(rows)]
+        moment_buf[pl.ds(me, 1)] = jnp.concatenate(mixed, axis=0)[None]
         wait = exchange(moment_buf, 2 * iteration + 1)
 
         if iteration == 0:
             base = (my_member * owned).astype(F32)
             wide = lax.broadcasted_iota(jnp.int32, (owned, LANES), 0).astype(F32) + base
 
-            @pl.loop(0, pairs)
-            def _(q):
-                even = row_buf[2 * q]
-                odd = row_buf[2 * q + 1]
-                slots = jnp.where(lane_row < half, pltpu.roll(even, half, 1), odd)
-                masks[0:batches, lane_tile(q)] = jnp.where(slot_col == slots, 1.0, 0.0).astype(jnp.bfloat16)
-                masks[batches : batches + owned, lane_tile(q)] = jnp.where(wide == slots, 1.0, 0.0).astype(jnp.bfloat16)
+            @pl.loop(0, devices // SUBS)
+            def _(c):
+                ids = jnp.concatenate([row_buf[c * SUBS + i] for i in range(SUBS)], axis=0)
+                stepped = pltpu.roll(ids, 0, 1, stride=rows, stride_axis=0)
+                for q in range(4):
+                    turned = pltpu.roll(stepped, (half - rows * q) % LANES, 1)
+                    slots = jnp.sum(jnp.where(lane // rows == sub, turned, 0.0), axis=0, keepdims=True)
+                    near[q * batches : (q + 1) * batches, lane_tile(c)] = jnp.where(
+                        slot_col == slots, 1.0, 0.0
+                    ).astype(jnp.bfloat16)
+                    own[q * owned : (q + 1) * owned, lane_tile(c)] = jnp.where(wide == slots, 1.0, 0.0).astype(
+                        jnp.bfloat16
+                    )
 
             for load in loads[3:]:
                 load.wait()
+
+        def base_step(step, carry):
+            for u in range(8):
+                t = step * 8 + u
+                part = coeff_col * (rho[:, lane_tile(t)] + mixing_beta * res[:, lane_tile(t)])
+                base_rows[pl.ds(t, 1), :] = jnp.sum(part, axis=0, keepdims=True)
+            return carry
+
+        lax.fori_loop(0, tiles // 8, base_step, 0)
         wait()
 
-        lane16 = lax.broadcasted_iota(jnp.int32, (2 * SUBS, LANES), 1)
-
-        @pl.loop(0, pairs)
-        def _(q):
-            even = moment_buf[2 * q]
-            odd = moment_buf[2 * q + 1]
-            first = jnp.where(lane16 < half, even, pltpu.roll(odd, half, 1))
-            second = jnp.where(lane16 < half, pltpu.roll(even, half, 1), odd)
-            rest = jnp.concatenate([first, second], axis=0)
-            for part in range(3):
-                piece = rest.astype(jnp.bfloat16)
-                mixed[part * 32 : (part + 1) * 32, lane_tile(q)] = piece
-                rest = rest - piece.astype(F32)
-
-        def gathered(start, count):
-            out = lax.dot_general(
-                mixed[...], masks[start : start + count, :], (((1,), (1,)), ((), ())), preferred_element_type=F32
-            )
-            return (out[0:32] + out[32:64] + out[64:96]) * scale
-
-        at_batch = gathered(0, batches)
+        everywhere = moment_buf[...].reshape(devices * rows, LANES)
+        pieces = jnp.concatenate([piece.astype(jnp.bfloat16) for piece in split(everywhere)], axis=1)
+
+        def gathered(mask, count):
+            out = jnp.dot(mask[...], pieces, preferred_element_type=F32)
+            out = out[:, 0:LANES] + out[:, LANES : 2 * LANES] + out[:, 2 * LANES :]
+            group = lax.broadcasted_iota(jnp.int32, (count, LANES), 1) // 32
+            total = out[0:count]
+            for q in range(1, 4):
+                total = jnp.where(group == q, out[q * count : (q + 1) * count], total)
+            total = total + pltpu.roll(total, 64, 1)
+            total = total + pltpu.roll(total, 32, 1)
+            return jnp.transpose(total)[0:32] * scale
+
+        at_batch = gathered(near, batches)
         comp = lax.broadcasted_iota(jnp.int32, (32, batches), 0)
         degree = sum((comp >= (l + 1) * (l + 1)).astype(F32) for l in range(4))
         damped = jnp.where(comp < harmonics, at_batch * (mixing_beta / (1.0 + degree)), 0.0)
@@ -302,18 +328,18 @@
                 col = jnp.sum(jnp.where(lane_b == b, damped, 0.0), axis=1, keepdims=True)
                 for v in range(per_batch):
                     t = b * per_batch + v
-                    part = coeff_col * (rho[:, lane_tile(t)] + mixing_beta * res[:, lane_tile(t)])
+                    part = col[24:32] * basis[24:25, lane_tile(t)]
                     for g in range(3):
-                        part = part - col[g * SUBS : (g + 1) * SUBS] * basis[g * SUBS : (g + 1) * SUBS, lane_tile(t)]
-                    part = part - col[24:32] * basis[24:25, lane_tile(t)]
-                    density_out[pl.ds(t, 1), :] = jnp.sum(part, axis=0, keepdims=True)
+                        part = part + col[g * SUBS : (g + 1) * SUBS] * basis[g * SUBS : (g + 1) * SUBS, lane_tile(t)]
+                    correct[pl.ds(t, 1), :] = jnp.sum(part, axis=0, keepdims=True)
             return carry
 
         lax.fori_loop(0, batches // 4, density_step, 0)
+        density = base_rows[...] - correct[...]
+        density_out[...] = density
         if last:
-            moments_out[...] = gathered(batches, owned)[0:harmonics]
+            moments_out[...] = gathered(own, owned)[0:harmonics]
         else:
-            density = density_out[...]
             new = target[...] + coupling[...] * jnp.tanh(density) - density
             fresh[...] = new
             fresh_w[...] = new * w[...]
@@ -350,15 +376,18 @@
             pltpu.VMEM(flat, F32),
             pltpu.VMEM(flat, F32),
             pltpu.VMEM((iters, devices, 1, LANES), F32),
-            pltpu.VMEM((iters, devices, 2 * SUBS, LANES), F32),
-            pltpu.VMEM((batches + owned, devices * batches), jnp.bfloat16),
-            pltpu.VMEM((96, devices * batches), jnp.bfloat16),
+            pltpu.VMEM((iters, devices, batches // 4, LANES), F32),
+            pltpu.VMEM((4 * batches, devices * batches // 4), jnp.bfloat16),
+            pltpu.VMEM((4 * owned, devices * batches // 4), jnp.bfloat16),
+            pltpu.VMEM((batches // 4, SUBS, LANES), F32),
+            pltpu.VMEM(flat, F32),
+            pltpu.VMEM(flat, F32),
             pltpu.SemaphoreType.DMA((6,)),
             pltpu.SemaphoreType.DMA((2 * iters, devices)),
             pltpu.SemaphoreType.DMA((2 * iters, devices)),
         ],
         compiler_params=pltpu.CompilerParams(
-            collective_id=0, has_side_effects=True, vmem_limit_bytes=48 * 1024 * 1024
+            collective_id=0, has_side_effects=True, vmem_limit_bytes=67043328
         ),
     )(
         batch_atom,

time: 55 us -> 43.9 us (0.80)
  local copies, waits for them, and re-layouts: 9.45 us -> 2.95 us
  Pallas kernels: 44.4 us -> 40 us
    unnamed x20 -> x2, local copies, waits for them, and re-layouts: 9.45 us -> 2.95 us
    pallas_call x1, Pallas kernels: 44.4 us -> 40 us  [local(): pl.pallas_call(functools.partial(kernel, cfg), out_shape=(jax.ShapeDtypeS...]
where the time goes in v2:
time: 43.9 us; the launch traced here: 43.6 us
  Pallas kernels  40 us (91%)
  local copies, waits for them, and re-layouts  2.95 us (7%)
  between operations  0.64 us (1%)
    pallas_call x1, Pallas kernels, local(): pl.pallas_call(functools.partial(kernel, cfg), out_shape=(jax.ShapeDtypeS...  40 us
    unnamed x2, local copies, waits for them, and re-layouts  2.95 us

profile of v2, /device:TPU:0, one launch (start us, length us, event | category | flops | bytes accessed | tf_op | source)
XLA Modules:
  0.0 43.6 jit_solution(5761171904421677477)
XLA Ops:
  0.6 40.0 %shard_map.104 = (f32[128,128]{1,0:T(8,128)}, f32[25,512]{1,0:T(8,128)}) custom-call(s32[64]{0:T(128)} %batch_atom.1, s32[2048]{0:T(1024)} %owner_slot.1, s32[2]{0:T(128)} %slot_index.1, f32[128,128]{1,0:T(8,128)} %bitcast.4, f32[128,128]{1,0:T(8,128)} %bitcast.5, f32[128,128]{1,0:T(8,128)} %bitcast.6, f32[25,16384]{1,0:T(8,128)} %basis_hbm.1, ...), custom_call_target="tpu_custom_call" | custom-call | tf_op jit(solution)/shard_map/pallas_call | solution.py:364
  40.7 1.5 %copy.13 = f32[16384]{0:T(1024)} copy(f32[16384]{0:T(1024)} %bitcast.7) | data formatting | bytes 131072
  42.2 1.5 %copy.14 = f32[25,512]{1,0:T(8,128)} copy(f32[25,512]{1,0:T(8,128)} %get-tuple-element.9) | data formatting | bytes 102400

commit v3 on v2

--- a/solution.py
+++ b/solution.py
@@ -314,27 +314,26 @@
                 total = jnp.where(group == q, out[q * count : (q + 1) * count], total)
             total = total + pltpu.roll(total, 64, 1)
             total = total + pltpu.roll(total, 32, 1)
-            return jnp.transpose(total)[0:32] * scale
+            return jnp.transpose(jnp.concatenate([total] * max(1, LANES // count), axis=0))[0:32] * scale
 
         at_batch = gathered(near, batches)
-        comp = lax.broadcasted_iota(jnp.int32, (32, batches), 0)
+        comp = lax.broadcasted_iota(jnp.int32, (32, LANES), 0)
         degree = sum((comp >= (l + 1) * (l + 1)).astype(F32) for l in range(4))
         damped = jnp.where(comp < harmonics, at_batch * (mixing_beta / (1.0 + degree)), 0.0)
-        lane_b = lax.broadcasted_iota(jnp.int32, (32, batches), 1)
-
-        def density_step(step, carry):
-            for u in range(4):
-                b = step * 4 + u
-                col = jnp.sum(jnp.where(lane_b == b, damped, 0.0), axis=1, keepdims=True)
+
+        def density_step(step, ahead):
+            for u in range(8):
+                b = step * 8 + u
+                col = jnp.broadcast_to(ahead[:, u : u + 1], (32, LANES))
                 for v in range(per_batch):
                     t = b * per_batch + v
                     part = col[24:32] * basis[24:25, lane_tile(t)]
                     for g in range(3):
                         part = part + col[g * SUBS : (g + 1) * SUBS] * basis[g * SUBS : (g + 1) * SUBS, lane_tile(t)]
                     correct[pl.ds(t, 1), :] = jnp.sum(part, axis=0, keepdims=True)
-            return carry
-
-        lax.fori_loop(0, batches // 4, density_step, 0)
+            return pltpu.roll(ahead, LANES - 8, 1)
+
+        lax.fori_loop(0, batches // 8, density_step, damped)
         density = base_rows[...] - correct[...]
         density_out[...] = density
         if last:

time: 43.9 us -> 42.6 us (0.970)
  Pallas kernels: 40 us -> 38.8 us
    pallas_call x1, Pallas kernels: 40 us -> 38.8 us  [local(): pl.pallas_call(functools.partial(kernel, cfg), out_shape=(jax.ShapeDtypeS...]
where the time goes in v3:
time: 42.6 us; the launch traced here: 42.4 us
  Pallas kernels  38.8 us (91%)
  local copies, waits for them, and re-layouts  2.95 us (7%)
  between operations  0.64 us (2%)
    pallas_call x1, Pallas kernels, local(): pl.pallas_call(functools.partial(kernel, cfg), out_shape=(jax.ShapeDtypeS...  38.8 us
    unnamed x2, local copies, waits for them, and re-layouts  2.95 us

profile of v3, /device:TPU:0, one launch (start us, length us, event | category | flops | bytes accessed | tf_op | source)
XLA Modules:
  0.0 42.4 jit_solution(184423594223579199)
XLA Ops:
  0.6 38.8 %shard_map.104 = (f32[128,128]{1,0:T(8,128)}, f32[25,512]{1,0:T(8,128)}) custom-call(s32[64]{0:T(128)} %batch_atom.1, s32[2048]{0:T(1024)} %owner_slot.1, s32[2]{0:T(128)} %slot_index.1, f32[128,128]{1,0:T(8,128)} %bitcast.4, f32[128,128]{1,0:T(8,128)} %bitcast.5, f32[128,128]{1,0:T(8,128)} %bitcast.6, f32[25,16384]{1,0:T(8,128)} %basis_hbm.1, ...), custom_call_target="tpu_custom_call" | custom-call | tf_op jit(solution)/shard_map/pallas_call | solution.py:363
  39.4 1.5 %copy.13 = f32[16384]{0:T(1024)} copy(f32[16384]{0:T(1024)} %bitcast.7) | data formatting | bytes 131072
  40.9 1.5 %copy.14 = f32[25,512]{1,0:T(8,128)} copy(f32[25,512]{1,0:T(8,128)} %get-tuple-element.9) | data formatting | bytes 102400

commit v4 on v3

--- a/solution.py
+++ b/solution.py
@@ -322,8 +322,8 @@
         damped = jnp.where(comp < harmonics, at_batch * (mixing_beta / (1.0 + degree)), 0.0)
 
         def density_step(step, ahead):
-            for u in range(8):
-                b = step * 8 + u
+            for u in range(16):
+                b = step * 16 + u
                 col = jnp.broadcast_to(ahead[:, u : u + 1], (32, LANES))
                 for v in range(per_batch):
                     t = b * per_batch + v
@@ -331,9 +331,9 @@
                     for g in range(3):
                         part = part + col[g * SUBS : (g + 1) * SUBS] * basis[g * SUBS : (g + 1) * SUBS, lane_tile(t)]
                     correct[pl.ds(t, 1), :] = jnp.sum(part, axis=0, keepdims=True)
-            return pltpu.roll(ahead, LANES - 8, 1)
-
-        lax.fori_loop(0, batches // 8, density_step, damped)
+            return pltpu.roll(ahead, LANES - 16, 1)
+
+        lax.fori_loop(0, batches // 16, density_step, damped)
         density = base_rows[...] - correct[...]
         density_out[...] = density
         if last:
@@ -342,6 +342,11 @@
             new = target[...] + coupling[...] * jnp.tanh(density) - density
             fresh[...] = new
             fresh_w[...] = new * w[...]
+
+
+def finish(density, moments, density_out, moments_out):
+    density_out[...] = density[...]
+    moments_out[...] = moments[...]
 
 
 def local(weights, target, coupling, multipole_basis, rho_hist, res_hist, batch_atom, owner_slot, slot_index):
@@ -399,6 +404,12 @@
         rho_hist,
         res_hist,
     )
+    density, moments = pl.pallas_call(
+        finish,
+        out_shape=(jax.ShapeDtypeStruct(flat, F32), jax.ShapeDtypeStruct((harmonics, owned), F32)),
+        in_specs=[vmem] * 2,
+        out_specs=(vmem, vmem),
+    )(density, moments)
     return density.reshape(points), moments
 
 

time: 42.6 us -> 40.5 us (0.951)
  local copies, waits for them, and re-layouts: 2.95 us -> 0 us
  Pallas kernels: 38.8 us -> 39.7 us
    unnamed x2 -> x0, local copies, waits for them, and re-layouts: 2.95 us -> none
    pallas_call x0 -> x1, Pallas kernels: none -> 1.53 us  [local(): pl.pallas_call(finish, out_shape=(jax.ShapeDtypeStruct(flat, F32), jax.Sh...]
    pallas_call x1, Pallas kernels: 38.8 us -> 38.2 us  [local(): pl.pallas_call(functools.partial(kernel, cfg), out_shape=(jax.ShapeDtypeS...]
where the time goes in v4:
time: 40.5 us; the launch traced here: 40.3 us
  Pallas kernels  39.7 us (98%)
  between operations  0.64 us (2%)
    pallas_call x1, Pallas kernels, local(): pl.pallas_call(functools.partial(kernel, cfg), out_shape=(jax.ShapeDtypeS...  38.2 us
    pallas_call x1, Pallas kernels, local(): pl.pallas_call(finish, out_shape=(jax.ShapeDtypeStruct(flat, F32), jax.Sh...  1.53 us

profile of v4, /device:TPU:0, one launch (start us, length us, event | category | flops | bytes accessed | tf_op | source)
XLA Modules:
  0.0 40.3 jit_solution(3696675166990799315)
XLA Ops:
  0.6 38.2 %shard_map.104 = (f32[128,128]{1,0:T(8,128)}, f32[25,512]{1,0:T(8,128)}) custom-call(s32[64]{0:T(128)} %batch_atom.1, s32[2048]{0:T(1024)} %owner_slot.1, s32[2]{0:T(128)} %slot_index.1, f32[128,128]{1,0:T(8,128)} %bitcast.4, f32[128,128]{1,0:T(8,128)} %bitcast.5, f32[128,128]{1,0:T(8,128)} %bitcast.6, f32[25,16384]{1,0:T(8,128)} %basis_hbm.1, ...), custom_call_target="tpu_custom_call" | custom-call | tf_op jit(solution)/shard_map/pallas_call | solution.py:368
  38.8 1.5 %shard_map.105 = (f32[128,128]{1,0:T(8,128)}, f32[25,512]{1,0:T(8,128)}) custom-call(f32[128,128]{1,0:T(8,128)} %get-tuple-element.6.density, f32[25,512]{1,0:T(8,128)} %get-tuple-element.7.moments), custom_call_target="tpu_custom_call" | custom-call | tf_op jit(solution)/shard_map/pallas_call | solution.py:407
